TPU v7x, 32 devices: a whole 2x2x4 slice. The times are simulated.
32 devices in a mesh: dp: 16 (over z, x, core), outer: 2 (over y).
Axes of the slice: x: 2, y: 2, z: 4, core: 2. Of those that a mesh axis runs over, the one named last changes fastest.
Arguments:
- images: bfloat16 [2048, 1024], P('dp'), may hold values from -8 to 8
- texts: bfloat16 [2048, 1024], P(('dp', 'outer')), may hold values from -8 to 8
- logit_scale: float32 [1], replicated, may hold values from 70 to 100
Outputs:
- image_loss: float32 [2048], P(('dp', 'outer'))
- text_loss: float32 [2048], P(('dp', 'outer'))
All inputs are finite; a program needn't handle non-finite values.
Results may differ from a plain program's by a relative error of at most 0.003.
Values may be sent and summed in bfloat16 or wider, within the bound.
A program may use at most 64 MiB of HBM per device.

v0:
```python
import functools

import jax
import jax.numpy as jnp
from jax import lax
from jax.experimental import pallas as pl
from jax.experimental.pallas import tpu as pltpu
from jax.sharding import PartitionSpec as P

MESH = pl.DeviceIdType.MESH
TEXT_CHUNKS = 2
IMAGE_CHUNKS = 2
LANES = 128
VMEM_BYTES = 66920448


def lane_partial(rows_a, rows_b):
    product = rows_a.astype(jnp.float32) * rows_b.astype(jnp.float32)
    total = product[:, :LANES]
    for start in range(LANES, product.shape[1], LANES):
        total = total + product[:, start : start + LANES]
    return total


def kernel(
    dims, scale_ref, img_hbm, txt_hbm, out,
    im, tx, im_scale, scores, st_i, st_t, got_i, got_t,
    load_sem, own_send, own_recv, tz_send, iz_send, x_send, y_send, d_send, tx_recv, im_recv,
    si_send, st_send, si_recv, st_recv,
):
    planes_i, planes_t, rows = dims
    t_piece, i_piece = rows // TEXT_CHUNKS, rows // IMAGE_CHUNKS
    me, y = lax.axis_index("dp"), lax.axis_index("outer")
    c, x, z = me % 2, (me // 2) % 2, me // 4
    p, group = z % planes_i, z // planes_i

    def at(zz, xx, cc, yy):
        return ((zz * 2 + xx) * 2 + cc, yy)

    def image_plane(pp):
        return group * planes_i + pp

    def text_plane(q):
        return q * planes_i + p

    def im_at(pp, k, h, ch):
        start = ((pp * 2 + k) * 2 + h) * rows + ch * i_piece
        return im.at[pl.ds(pl.multiple_of(start, i_piece), i_piece)]

    def im_shard(k):
        return im.at[pl.ds(pl.multiple_of((p * 2 + k) * 2 * rows, 2 * rows), 2 * rows)]

    def tx_at(q, xs, ch):
        return tx.at[pl.ds(pl.multiple_of((q * 2 + xs) * rows + ch * t_piece, t_piece), t_piece)]

    def tx_shard(xs):
        return tx.at[pl.ds(pl.multiple_of((group * 2 + xs) * rows, rows), rows)]

    def rc(src, dst, ss, rs, dev):
        return pltpu.make_async_remote_copy(
            src_ref=src, dst_ref=dst, send_sem=ss, recv_sem=rs, device_id=dev, device_id_type=MESH
        )

    img_load = pltpu.make_async_copy(img_hbm, im_shard(c), load_sem.at[0])
    txt_load = pltpu.make_async_copy(txt_hbm, tx_shard(x), load_sem.at[1])
    img_load.start()
    txt_load.start()

    barrier = pltpu.get_barrier_semaphore()
    partners = [at(text_plane((group + d) % planes_t), x, c, y) for d in range(1, planes_t)]
    partners += [at(image_plane((p + d) % planes_i), x, c, y) for d in range(1, planes_i)]
    partners += [at(z, 1 - x, c, y), at(z, x, c, 1 - y), at(z, x, 1 - c, y)]
    for dev in partners:
        pl.semaphore_signal(barrier, inc=1, device_id=dev, device_id_type=MESH)
    img_load.wait()
    txt_load.wait()
    pl.semaphore_wait(barrier, len(partners))

    def text_z(d, ch):
        return rc(tx_at(group, x, ch), tx_at(group, x, ch), tz_send.at[d - 1, ch],
                  tx_recv.at[group, x, ch], at(text_plane((group + d) % planes_t), x, c, y))

    def text_x_own(xs):
        return rc(tx_shard(xs), tx_shard(xs), own_send.at[0], own_recv.at[0], at(z, 1 - x, c, y))

    def text_x(d, xs, ch):
        q = (group + d) % planes_t
        return rc(tx_at(q, xs, ch), tx_at(q, xs, ch), x_send.at[d - 1, ch],
                  tx_recv.at[q, xs, ch], at(z, 1 - x, c, y))

    def image_z(d, ch):
        return rc(im_at(p, c, y, ch), im_at(p, c, y, ch), iz_send.at[d - 1, ch],
                  im_recv.at[p, c, y, ch], at(image_plane((p + d) % planes_i), x, c, y))

    def image_y(d, h, ch):
        pp = (p + d) % planes_i
        return rc(im_at(pp, c, h, ch), im_at(pp, c, h, ch), y_send.at[d - 1, ch],
                  im_recv.at[pp, c, h, ch], at(z, x, c, 1 - y))

    def image_d_own(k):
        return rc(im_shard(k), im_shard(k), own_send.at[1], own_recv.at[1], at(z, x, 1 - c, y))

    def image_d(d, k, h, ch):
        pp = (p + d) % planes_i
        return rc(im_at(pp, k, h, ch), im_at(pp, k, h, ch), d_send.at[d - 1, h, ch],
                  im_recv.at[pp, k, h, ch], at(z, x, 1 - c, y))

    for ch in range(IMAGE_CHUNKS):
        for d in range(1, planes_i):
            image_z(d, ch).start()
    for ch in range(TEXT_CHUNKS):
        for d in range(1, planes_t):
            text_z(d, ch).start()
    text_x_own(x).start()
    image_d_own(c).start()

    def pass_text(ch):
        for d in range(1, planes_t):
            copy = text_x(d, x, ch)
            copy.wait_recv()
            copy.start()

    def pass_image(ch):
        for d in range(1, planes_i):
            copy = image_y(d, y, ch)
            copy.wait_recv()
            copy.start()
            image_d(d, c, y, ch).start()

    def pass_to_core(ch):
        for d in range(1, planes_i):
            image_y(d, 1 - y, ch).wait_recv()
            image_d(d, c, 1 - y, ch).start()

    per = TEXT_CHUNKS // IMAGE_CHUNKS
    inner = p != group % 2

    @pl.when(inner)
    def _():
        for ch in range(IMAGE_CHUNKS):
            pass_image(ch)
        for ch in range(TEXT_CHUNKS):
            pass_text(ch)
            if ch < IMAGE_CHUNKS:
                pass_to_core(ch)

    @pl.when(jnp.logical_not(inner))
    def _():
        for ch in range(TEXT_CHUNKS):
            pass_text(ch)
            if ch % per == per - 1:
                pass_image(ch // per)
        for ch in range(IMAGE_CHUNKS):
            pass_to_core(ch)

    factor = scale_ref[0]
    wide, deep = 2 * rows, 4 * rows

    def im_rows(pp):
        return pl.ds(pl.multiple_of(pp * deep, deep), deep)

    def scale_images(pp):
        images = im[im_rows(pp), :]
        total = jnp.sum(lane_partial(images, images), axis=1, keepdims=True)
        im_scale[im_rows(pp), :] = jnp.broadcast_to(lax.rsqrt(total + 1.0) * factor, (deep, wide))

    def read_texts(q):
        texts = tx[pl.ds(pl.multiple_of(q * wide, wide), wide), :]
        total = jnp.sum(jnp.transpose(lane_partial(texts, texts)), axis=0, keepdims=True)
        return texts, lax.rsqrt(total + 1.0)

    def score(pp, q, texts, text_scale):
        block = lax.dot_general(
            im[im_rows(pp), :], texts, (((1,), (1,)), ((), ())), preferred_element_type=jnp.float32
        )
        block = block * im_scale[im_rows(pp), :] * text_scale
        scores[im_rows(pp), pl.ds(pl.multiple_of(q * wide, wide), wide)] = block

    def text_stats(q):
        block = scores[:, pl.ds(pl.multiple_of(q * wide, wide), wide)]
        peak = jnp.max(block, axis=0, keepdims=True)
        lse = peak + jnp.log(jnp.sum(jnp.exp(block - peak), axis=0, keepdims=True))
        st_t[q] = jnp.broadcast_to(lse, (8, wide))

    def stat_t(q, xs):
        return rc(st_t.at[q], got_t.at[group * 2 + x], st_send.at[q, xs],
                  st_recv.at[group * 2 + x], at(text_plane(q), xs, c, y))

    def stat_i(pp, k, h):
        slot = (p * 2 + y) * 2 + c
        return rc(st_i.at[pp * 2 + k], got_i.at[slot], si_send.at[pp, k, h],
                  si_recv.at[slot], at(image_plane(pp), x, k, h))

    t_pairs = [(q, xs) for q in range(planes_t) for xs in range(2)]
    i_triples = [(pp, k, h) for pp in range(planes_i) for k in range(2) for h in range(2)]

    def t_self(q, xs):
        return jnp.logical_and(text_plane(q) == z, xs == x)

    def i_self(pp, k, h):
        return (pp * 2 + k) * 2 + h == (p * 2 + c) * 2 + y

    def send_text_stats(q, xs):
        mine = t_self(q, xs)

        @pl.when(jnp.logical_not(mine))
        def _():
            stat_t(q, xs).start()

        @pl.when(mine)
        def _():
            got_t[group * 2 + x] = st_t[q]

    image_d_own(1 - c).wait_recv()
    scale_images(p)
    text_x_own(1 - x).wait_recv()
    own_texts = read_texts(group)
    score(p, group, *own_texts)
    for d in range(1, planes_i):
        for h in range(2):
            for ch in range(IMAGE_CHUNKS):
                image_d(d, 1 - c, h, ch).wait_recv()
        pp = (p + d) % planes_i
        scale_images(pp)
        score(pp, group, *own_texts)
    text_stats(group)
    for xs in range(2):
        send_text_stats(group, xs)
    for d in range(1, planes_t):
        for ch in range(TEXT_CHUNKS):
            text_x(d, 1 - x, ch).wait_recv()
        q = (group + d) % planes_t
        texts = read_texts(q)
        for pp in range(planes_i):
            score(pp, q, *texts)
        text_stats(q)
        for xs in range(2):
            send_text_stats(q, xs)

    for s in range(planes_i * 2):
        block = scores[pl.ds(s * 2 * rows, 2 * rows), :]
        peak = jnp.max(block, axis=1, keepdims=True)
        lse = peak + jnp.log(jnp.sum(jnp.exp(block - peak), axis=1, keepdims=True))
        st_i[s] = jnp.transpose(jnp.broadcast_to(lse, (2 * rows, LANES)))[:8, :]

    for pp, k, h in i_triples:
        mine = i_self(pp, k, h)

        @pl.when(jnp.logical_not(mine))
        def _():
            stat_i(pp, k, h).start()

        @pl.when(mine)
        def _():
            got_i[(p * 2 + y) * 2 + c] = st_i[pp * 2 + k]

    own_img = im[pl.ds(pl.multiple_of(((p * 2 + c) * 2 + y) * rows, rows), rows), :]
    own_txt = tx[pl.ds(pl.multiple_of((group * 2 + x) * rows, rows), rows), :]

    def row_sum(a, b):
        return jnp.sum(jnp.transpose(lane_partial(a, b)), axis=0, keepdims=True)

    diagonal = (
        row_sum(own_img, own_txt)
        * lax.rsqrt(row_sum(own_img, own_img) + 1.0)
        * lax.rsqrt(row_sum(own_txt, own_txt) + 1.0)
        * factor
    )

    text_x_own(x).wait_send()
    image_d_own(c).wait_send()
    for ch in range(TEXT_CHUNKS):
        for d in range(1, planes_t):
            text_z(d, ch).wait_send()
            text_x(d, x, ch).wait_send()
    for ch in range(IMAGE_CHUNKS):
        for d in range(1, planes_i):
            image_z(d, ch).wait_send()
            image_y(d, y, ch).wait_send()
            for h in range(2):
                image_d(d, c, h, ch).wait_send()

    def merge(got, count):
        parts = [got[s][0:1, :] for s in range(count)]
        peak = functools.reduce(jnp.maximum, parts)
        total = functools.reduce(jnp.add, [jnp.exp(part - peak) for part in parts])
        return peak + jnp.log(total)

    for s in range(planes_i * 4):

        @pl.when(s != (p * 2 + y) * 2 + c)
        def _():
            rc(st_i.at[0], got_i.at[s], si_send.at[0, 0, 0], si_recv.at[s], at(z, x, 1 - c, y)).wait_recv()

    lse = merge(got_i, planes_i * 4)
    out[0:1, :] = jnp.where(y == 0, lse[:, :rows], lse[:, rows:]) - diagonal

    for s in range(planes_t * 2):

        @pl.when(s != group * 2 + x)
        def _():
            rc(st_t.at[0], got_t.at[s], st_send.at[0, 0], st_recv.at[s], at(z, x, 1 - c, y)).wait_recv()

    lse = merge(got_t, planes_t * 2)
    out[1:2, :] = jnp.where(x == 0, lse[:, :rows], lse[:, rows:]) - diagonal

    for q, xs in t_pairs:

        @pl.when(jnp.logical_not(t_self(q, xs)))
        def _():
            stat_t(q, xs).wait_send()

    for pp, k, h in i_triples:

        @pl.when(jnp.logical_not(i_self(pp, k, h)))
        def _():
            stat_i(pp, k, h).wait_send()


def on_device(planes_i, planes_t, images, texts, logit_scale):
    rows, width = texts.shape
    dma = pltpu.SemaphoreType.DMA
    f32 = jnp.float32
    losses = pl.pallas_call(
        functools.partial(kernel, (planes_i, planes_t, rows)),
        out_shape=jax.ShapeDtypeStruct((2, rows), f32),
        in_specs=[
            pl.BlockSpec(memory_space=pltpu.SMEM),
            pl.BlockSpec(memory_space=pltpu.HBM),
            pl.BlockSpec(memory_space=pltpu.HBM),
        ],
        out_specs=pl.BlockSpec(memory_space=pltpu.VMEM),
        scratch_shapes=[
            pltpu.VMEM((planes_i * 4 * rows, width), images.dtype),
            pltpu.VMEM((planes_t * 2 * rows, width), texts.dtype),
            pltpu.VMEM((planes_i * 4 * rows, 2 * rows), f32),
            pltpu.VMEM((planes_i * 4 * rows, planes_t * 2 * rows), f32),
            pltpu.VMEM((planes_i * 2, 8, 2 * rows), f32),
            pltpu.VMEM((planes_t, 8, 2 * rows), f32),
            pltpu.VMEM((planes_i * 4, 8, 2 * rows), f32),
            pltpu.VMEM((planes_t * 2, 8, 2 * rows), f32),
            dma((2,)),
            dma((2,)),
            dma((2,)),
            dma((planes_t, TEXT_CHUNKS)),
            dma((planes_i, IMAGE_CHUNKS)),
            dma((planes_t, TEXT_CHUNKS)),
            dma((planes_i, IMAGE_CHUNKS)),
            dma((planes_i, 2, IMAGE_CHUNKS)),
            dma((planes_t, 2, TEXT_CHUNKS)),
            dma((planes_i, 2, 2, IMAGE_CHUNKS)),
            dma((planes_i, 2, 2)),
            dma((planes_t, 2)),
            dma((planes_i * 4,)),
            dma((planes_t * 2,)),
        ],
        compiler_params=pltpu.CompilerParams(
            collective_id=0, has_side_effects=True, vmem_limit_bytes=VMEM_BYTES
        ),
    )(logit_scale, images, texts)
    return losses[0], losses[1]


def solution(mesh):
    planes = mesh.shape["dp"] // 4
    planes_i = max(d for d in range(1, planes + 1) if planes % d == 0 and d * d <= planes)
    in_specs = (P("dp", None), P(("dp", "outer"), None), P())
    out_specs = (P(("dp", "outer")), P(("dp", "outer")))
    return jax.shard_map(
        functools.partial(on_device, planes_i, planes // planes_i),
        mesh=mesh, in_specs=in_specs, out_specs=out_specs, check_vma=False,
    )
```

profile of v0, /device:TPU:0, one launch (start us, length us, event | category | flops | bytes accessed | tf_op | source)
XLA Modules:
  0.0 24.2 jit_solution(4691700409056118043)
XLA Ops:
  1.3 21.7 %shard_map.50 = f32[2,64]{1,0:T(2,128)} custom-call(f32[1]{0:T(128)S(6)} %copy.5.scale_ref, bf16[128,1024]{1,0:T(8,128)(2,1)} %img_hbm.1, bf16[64,1024]{1,0:T(8,128)(2,1)} %txt_hbm.1), custom_call_target="tpu_custom_call" | custom-call | tf_op jit(solution)/shard_map/pallas_call | solution.py:324
  23.0 1.3 %slice_bitcast_fusion = (f32[64]{0:T(128)}, f32[64]{0:T(128)}) fusion(f32[2,64]{1,0:T(2,128)} %shard_map.50), kind=kLoop, calls=%fused_computation | loop fusion | bytes 1024 | tf_op jit(solution)/shard_map/squeeze | solution.py:361
where the time goes:
time: 24.4 us; the launch traced here: 24.2 us
  Pallas kernels  21.7 us (89%)
  between operations  1.28 us (5%)
  local copies, waits for them, and re-layouts  1.25 us (5%)
    pallas_call x1, Pallas kernels, on_device(): pl.pallas_call(functools.partial(kernel, (planes_i, planes_t, rows)), out...  21.7 us
    squeeze x1, local copies, waits for them, and re-layouts, on_device(): return (losses[0], losses[1])  1.25 us

commit v1 on v0

--- a/solution.py
+++ b/solution.py
@@ -323,7 +323,7 @@
     f32 = jnp.float32
     losses = pl.pallas_call(
         functools.partial(kernel, (planes_i, planes_t, rows)),
-        out_shape=jax.ShapeDtypeStruct((2, rows), f32),
+        out_shape=pltpu.VMEM((2, rows), f32),
         in_specs=[
             pl.BlockSpec(memory_space=pltpu.SMEM),
             pl.BlockSpec(memory_space=pltpu.HBM),

time: 24.4 us -> 23.1 us (0.947)
  local copies, waits for them, and re-layouts: 1.25 us -> 0.52 us
  Pallas kernels: 21.7 us -> 21.1 us
    squeeze x1, local copies, waits for them, and re-layouts: 1.25 us -> 0.52 us  [on_device(): return (losses[0], losses[1])]
    pallas_call x1, Pallas kernels: 21.7 us -> 21.1 us  [on_device(): pl.pallas_call(functools.partial(kernel, (planes_i, planes_t, rows)), out...]
where the time goes in v1:
time: 23.1 us; the launch traced here: 22.9 us
  Pallas kernels  21.1 us (91%)
  between operations  1.28 us (6%)
  local copies, waits for them, and re-layouts  0.52 us (2%)
    pallas_call x1, Pallas kernels, on_device(): pl.pallas_call(functools.partial(kernel, (planes_i, planes_t, rows)), out...  21.1 us
    squeeze x1, local copies, waits for them, and re-layouts, on_device(): return (losses[0], losses[1])  0.52 us

profile of v1, /device:TPU:0, one launch (start us, length us, event | category | flops | bytes accessed | tf_op | source)
XLA Modules:
  0.0 22.9 jit_solution(14125533980230322123)
XLA Ops:
  1.3 21.1 %shard_map.50 = f32[2,64]{1,0:T(2,128)S(1)} custom-call(f32[1]{0:T(128)S(6)} %copy.5.scale_ref, bf16[128,1024]{1,0:T(8,128)(2,1)} %img_hbm.1, bf16[64,1024]{1,0:T(8,128)(2,1)} %txt_hbm.1), custom_call_target="tpu_custom_call" | custom-call | tf_op jit(solution)/shard_map/pallas_call | solution.py:324
  22.4 0.5 %slice_bitcast_fusion = (f32[64]{0:T(128)}, f32[64]{0:T(128)}) fusion(f32[2,64]{1,0:T(2,128)S(1)} %shard_map.50), kind=kLoop, calls=%fused_computation | loop fusion | bytes 1024 | tf_op jit(solution)/shard_map/squeeze | solution.py:361
